TPU v7x, 32 devices: a whole 2x2x4 slice. The times are simulated.
32 devices in a mesh: groups: 2 (over y), seq: 4 (over z), head: 2 (over x), rep: 2 (over core).
Axes of the slice: x: 2, y: 2, z: 4, core: 2. Of those that a mesh axis runs over, the one named last changes fastest.
Arguments:
- queries: bfloat16 [2048, 6144], P(('groups', 'seq', 'rep'), 'head'), parts along dimension 0, may hold values from -150 to 150
- key_tokens: bfloat16 [2048, 6144], P(('groups', 'seq', 'rep'), 'head'), parts along dimension 0, may hold values from -6 to 6
- value_tokens: bfloat16 [2048, 6144], P(('groups', 'seq', 'rep'), 'head'), parts along dimension 0, may hold values from -6 to 6
- stream: bfloat16 [2048, 6144], P(('groups', 'seq', 'rep'), 'head'), parts along dimension 0, may hold values from -6 to 6
- norm_gain: float32 [6144], P('head'), may hold values from 0.1 to 1.9
- latent_weight: bfloat16 [6144, 64], P('head'), may hold values from -0.078125 to 0.078125
- tile_pool: bfloat16 [8, 64, 2, 128], P(('groups', 'seq')), parts along dimension 0, may hold values from -6 to 6
- tile_position: int32 [8], P('groups'), parts along dimension 0, may hold values from 0 to 3, each once
- lift_weight: bfloat16 [64, 512], P(None, ('head', 'rep')), may hold values from -0.75 to 0.75
- lift_bias: float32 [512], P(('head', 'rep')), may hold values from -3 to 3
- conv_weight: bfloat16 [2, 27, 512, 512], P(None, None, ('head', 'rep')), may hold values from -0.0546875 to 0.0546875
Outputs:
- hidden: bfloat16 [2048, 6144], P(('groups', 'seq', 'rep'), 'head'), parts along dimension 0
- latents: float32 [2048, 64], P(('groups', 'seq', 'rep')), parts along dimension 0
- decoded: float32 [1024, 2, 4, 128], P(('groups', 'head', 'rep'), None, 'seq'), parts along dimension 0
There are 2 independent parts, one for each index of `groups`. A program takes and returns all parts, laid end to end along the dimension named above; an argument that names none is the same for every part. Nothing has to cross between parts.
Inputs may be any that keep to these rules, and one draw needn't show every extreme that they name: `tile_position`: each of the 4 grid rows is named by exactly one pool tile.
All inputs are finite; a program needn't handle non-finite values.
Results may differ from a plain program's by a relative error of at most 0.01.
Values may be sent and summed in bfloat16 or wider, within the bound.
A program may use at most 128 MiB of HBM per device.

v0:
```python
import math

import jax
import jax.numpy as jnp
from jax import lax
from jax.sharding import PartitionSpec as P

HEAD_DIM = 128
WIDTH = 6144


epsilon = 1e-06
negative = -1e30


def padded(shard, sides, width):
    for axis, dim in sides:
        peers, length = (lax.axis_size(axis), shard.shape[dim])
        up = [(i, (i + 1) % peers) for i in range(peers - 1)]
        down = [(j, i) for i, j in up]
        last = lax.slice_in_dim(shard, length - width, length, axis=dim)
        leading = lax.slice_in_dim(shard, 0, width, axis=dim)
        before = lax.ppermute(last, axis, up)
        after = lax.ppermute(leading, axis, down)
        shard = jnp.concatenate([before, shard, after], axis=dim)
    return shard


def prepare(block_rows):
    row_count = block_rows.shape[0]
    head_count = block_rows.shape[1] // HEAD_DIM
    query_heads = block_rows.reshape(row_count, head_count, HEAD_DIM)
    initial = (
        jnp.full((head_count, row_count), negative, jnp.float32),
        jnp.zeros((head_count, row_count), jnp.float32),
        jnp.zeros((head_count, row_count, HEAD_DIM), jnp.float32),
    )
    return (query_heads, initial)


def make_update(query_heads, state, pieces):
    head_count = query_heads.shape[1]
    factor = 1.0 / math.sqrt(HEAD_DIM)
    running_max, running_sum, accum = state
    key_piece, value_piece = pieces
    piece_rows = key_piece.shape[0]
    key_heads = key_piece.reshape(piece_rows, head_count, HEAD_DIM)
    value_heads = value_piece.reshape(piece_rows, head_count, HEAD_DIM)
    scores = (
        jnp.einsum("qhd,khd->hqk", query_heads, key_heads, preferred_element_type=jnp.float32)
        * factor
    )
    new_max = jnp.maximum(running_max, jnp.max(scores, axis=2))
    exponent = jnp.exp(scores - new_max[:, :, None])
    running_sum = jnp.sum(exponent, axis=2)
    accum = jnp.einsum(
        "hqk,khd->hqd",
        exponent.astype(jnp.bfloat16),
        value_heads,
        preferred_element_type=jnp.float32,
    )
    return (new_max, running_sum, accum)


def finish(state):
    running_max, running_sum, accum = state
    result = accum / running_sum[:, :, None]
    return jnp.transpose(result, (1, 0, 2)).reshape(result.shape[1], -1).astype(jnp.bfloat16)


def shift_columns(window, col_shift):
    if col_shift == 0:
        return window
    edge = jnp.zeros(window.shape[:-1] + (1,), window.dtype)
    if col_shift < 0:
        return jnp.concatenate([edge, window[..., :-1]], axis=-1)
    return jnp.concatenate([window[..., 1:], edge], axis=-1)


def tap_sum(running, piece_block, layer_weight):
    piece_rows = piece_block.shape[0]
    frames = piece_block.shape[1]
    band_rows = piece_block.shape[2] - 2
    framed = jnp.pad(piece_block, ((0, 0), (1, 1), (0, 0), (0, 0)))
    for frame_off in range(3):
        for row_off in range(3):
            for col_off in range(3):
                window = shift_columns(
                    framed[:, frame_off : frame_off + frames, row_off : row_off + band_rows, :],
                    col_off - 1,
                )
                tap_weight = layer_weight[frame_off * 9 + row_off * 3 + col_off]
                running = running + lax.dot_general(
                    tap_weight,
                    window.reshape(piece_rows, -1),
                    (((1,), (0,)), ((), ())),
                    preferred_element_type=jnp.float32,
                )
    return running


def make_pick(tile_position, own_rows, piece_block):
    selector = (own_rows[:, None] == tile_position[None, :]).astype(jnp.bfloat16)
    return jnp.einsum("tp,plfc->lftc", selector, piece_block, preferred_element_type=jnp.float32)


def shards(
    queries,
    key_tokens,
    value_tokens,
    stream,
    norm_gain,
    latent_weight,
    tile_pool,
    tile_position,
    lift_weight,
    lift_bias,
    conv_weight,
):
    query_heads, initial = prepare(queries)
    state = make_update(
        query_heads,
        initial,
        (
            lax.all_gather(key_tokens, ("seq", "rep"), axis=0, tiled=True),
            lax.all_gather(value_tokens, ("seq", "rep"), axis=0, tiled=True),
        ),
    )
    attended = finish(state)
    combined = stream.astype(jnp.float32) + attended.astype(jnp.float32)
    hidden = combined.astype(jnp.bfloat16)
    widened = hidden.astype(jnp.float32)
    scaled = (widened * norm_gain).astype(jnp.bfloat16)
    partial_proj = jnp.dot(scaled, latent_weight, preferred_element_type=jnp.float32)
    partial_squares = jnp.sum(widened * widened, axis=1)
    projected, squares = (
        lax.psum(partial_proj.astype(jnp.bfloat16), "head").astype(jnp.float32),
        lax.psum(partial_squares.astype(jnp.bfloat16), "head").astype(jnp.float32),
    )
    latents = projected * lax.rsqrt(squares / WIDTH + epsilon)[:, None]
    tiles_here = tile_pool.shape[0]
    frames = tile_pool.shape[2]
    columns = tile_pool.shape[3]
    own_rows = lax.axis_index("seq") * tiles_here + jnp.arange(tiles_here, dtype=jnp.int32)
    collected = make_pick(
        tile_position, own_rows, lax.all_gather(tile_pool, "seq", axis=0, tiled=True)
    )
    latent_grid = collected.astype(jnp.bfloat16)
    channels_here = lift_weight.shape[1]
    feature_map = (
        lax.dot_general(
            lift_weight,
            latent_grid.reshape(latent_grid.shape[0], -1),
            (((0,), (0,)), ((), ())),
            preferred_element_type=jnp.float32,
        )
        + lift_bias[:, None]
    )
    for layer_index in range(conv_weight.shape[0]):
        layer_weight = conv_weight[layer_index]
        active = (
            jax.nn.silu(feature_map)
            .astype(jnp.bfloat16)
            .reshape(channels_here, frames, tiles_here, columns)
        )
        zeros_here = jnp.zeros(feature_map.shape, jnp.float32)
        bordered = padded(active, (("seq", 2),), 1)
        rimmed = lax.all_gather(bordered, ("head", "rep"), axis=0, tiled=True)
        update = tap_sum(zeros_here, rimmed, layer_weight)
        feature_map = feature_map + update
    decoded = feature_map.reshape(channels_here, frames, tiles_here, columns)
    return (hidden, latents, decoded)


def solution(mesh):
    in_specs = (
        P(("groups", "seq", "rep"), "head"),
        P(("groups", "seq", "rep"), "head"),
        P(("groups", "seq", "rep"), "head"),
        P(("groups", "seq", "rep"), "head"),
        P("head"),
        P("head", None),
        P(("groups", "seq"), None, None, None),
        P("groups"),
        P(None, ("head", "rep")),
        P(("head", "rep")),
        P(None, None, ("head", "rep"), None),
    )
    out_specs = (
        P(("groups", "seq", "rep"), "head"),
        P(("groups", "seq", "rep"), None),
        P(("groups", "head", "rep"), None, "seq", None),
    )
    return jax.shard_map(shards, mesh=mesh, in_specs=in_specs, out_specs=out_specs, check_vma=False)
```

profile of v0, /device:TPU:0, one launch (start us, length us, event | category | flops | bytes accessed | tf_op | source)
XLA Modules:
  0.0 183.7 jit_solution(11316770356860687936)
XLA Ops:
  7.2 2.3 %copy.24 = bf16[128,3072]{0,1:T(8,128)(2,1)} copy(bf16[128,3072]{1,0:T(8,128)(2,1)} %param.12) | data formatting | bytes 1572864 | tf_op args[1]
  9.7 0.8 copy.29
  10.4 15.2 %all_gather.17 = bf16[4,64,2,128]{3,1,2,0:T(8,128)(2,1)S(1)} all-gather(bf16[1,64,2,128]{3,1,2,0:T(8,128)(2,1)S(1)} %copy.29), channel_id=1, replica_groups=mesh['groups'=2,'seq'=4,'head'=2,'rep'=2] {'seq'}, dimensions={0}, use_global_device_ids=true | all-gather | bytes 163840 | tf_op jit(solution)/shard_map/all_gather | solution.py:146
  25.6 0.9 fusion.151
  26.5 0.9 multiply_convert_fusion.1
  27.4 1.3 collective-permute-start.1
  28.7 9.4 %collective-permute-start = (bf16[128,2,1,128]{0,3,1,2:T(8,128)(2,1)S(1)}, bf16[128,2,1,128]{0,3,1,2:T(8,128)(2,1)S(1)}, u32[]{:S(2)}, u32[]{:S(2)}) collective-permute-start(bf16[128,2,1,128]{0,3,1,2:T(8,128)(2,1)S(1)} %bitcast.462), channel_id=1, source_target_pairs={{0,4},{4,8},{8,12},{1,5},{5,9},{9,13},{2,6},{6,10},{10,14},{3,7},{... | collective-permute-start | bytes 196616 | tf_op jit(solution)/shard_map/ppermute | solution.py:23
  38.2 6.8 %collective-permute-done.1 = bf16[128,2,1,128]{0,3,1,2:T(8,128)(2,1)S(1)} collective-permute-done((bf16[128,2,1,128]{0,3,1,2:T(8,128)(2,1)S(1)}, bf16[128,2,1,128]{0,3,1,2:T(8,128)(2,1)S(1)}, u32[]{:S(2)}, u32[]{:S(2)}) %collective-permute-start.1) | collective-permute-done | bytes 65568 | tf_op jit(solution)/shard_map/ppermute | solution.py:24
  45.1 8.6 %all_gather.18 = bf16[512,2,3,128]{0,3,1,2:T(8,128)(2,1)S(1)} all-gather(bf16[128,2,3,128]{0,3,1,2:T(8,128)(2,1)S(1)} %pad_maximum_fusion), channel_id=1, replica_groups=mesh['groups'=2,'seq'=4,'head'=2,'rep'=2] {'head','rep'}, dimensions={0}, use_global_device_ids=true | all-gather | bytes 983040 | tf_op jit(solution)/shard_map/all_gather | solution.py:168
  55.1 0.9 slice-done
  56.0 1.0 slice-done.1
  63.5 1.3 collective-permute-start.3
  64.8 4.5 %collective-permute-start.2 = (bf16[128,2,1,128]{0,3,1,2:T(8,128)(2,1)S(1)}, bf16[128,2,1,128]{0,3,1,2:T(8,128)(2,1)S(1)}, u32[]{:S(2)}, u32[]{:S(2)}) collective-permute-start(bf16[128,2,1,128]{0,3,1,2:T(8,128)(2,1)S(1)} %bitcast.465), channel_id=1, source_target_pairs={{0,4},{4,8},{8,12},{1,5},{5,9},{9,13},{2,6},{6,10},{10,14},{3,7},{... | collective-permute-start | bytes 196616 | tf_op jit(solution)/shard_map/ppermute | solution.py:23
  69.4 5.8 %collective-permute-done.3 = bf16[128,2,1,128]{0,3,1,2:T(8,128)(2,1)S(1)} collective-permute-done((bf16[128,2,1,128]{0,3,1,2:T(8,128)(2,1)S(1)}, bf16[128,2,1,128]{0,3,1,2:T(8,128)(2,1)S(1)}, u32[]{:S(2)}, u32[]{:S(2)}) %collective-permute-start.3) | collective-permute-done | bytes 65568 | tf_op jit(solution)/shard_map/ppermute | solution.py:24
  75.2 8.7 %all_gather.19 = bf16[512,2,3,128]{0,3,1,2:T(8,128)(2,1)S(1)} all-gather(bf16[128,2,3,128]{0,3,1,2:T(8,128)(2,1)S(1)} %pad_maximum_fusion.1), channel_id=1, replica_groups=mesh['groups'=2,'seq'=4,'head'=2,'rep'=2] {'head','rep'}, dimensions={0}, use_global_device_ids=true | all-gather | bytes 983040 | tf_op jit(solution)/shard_map/all_gather | solution.py:168
  92.7 4.7 %multiply_reduce_fusion = (f32[24,128]{1,0:T(8,128)S(1)}, f32[24,128,1024]{2,1,0:T(8,128)S(1)}) fusion(bf16[1024,24,128]{0,2,1:T(8,128)(2,1)} %bitcast.401, bf16[128,3072]{1,0:T(8,128)(2,1)S(1)} %copy-done), kind=kOutput, calls=%fused_computation.1 | convolution fusion | flops 811594752 | bytes 19673088 | tf_op jit(solution)/shard_map/qhd,khd->hqk/dot_general | solution.py:50
  97.4 4.5 %copy-done.2 = f32[24,128,1024]{2,1,0:T(8,128)} copy-done((f32[24,128,1024]{2,1,0:T(8,128)}, f32[24,128,1024]{2,1,0:T(8,128)S(1)}, u32[]{:S(2)}) %copy-start.2) | copy-done | bytes 12582936
  101.9 2.8 %fusion = f32[24,128]{1,0:T(8,128)S(1)} fusion(f32[24,128,1024]{2,1,0:T(8,128)S(1)} %get-tuple-element.71, f32[24,128]{1,0:T(8,128)S(1)} %broadcast_maximum_fusion), kind=kLoop, calls=%fused_computation.2 | loop fusion | flops 9434112 | bytes 12607488 | tf_op jit(solution)/shard_map/reduce_sum | solution.py:55
  104.7 41.2 %all-gather.5.cloned.1.call-done = bf16[1024,3072]{1,0:T(8,128)(2,1)} async-done(((bf16[128,3072]{1,0:T(8,128)(2,1)}), bf16[1024,3072]{1,0:T(8,128)(2,1)}) %all-gather.5.cloned.1.call-update) | async-done | bytes 6291472 | tf_op jit(solution)/shard_map/all_gather | solution.py:126
  145.9 8.7 %copy.27 = bf16[1024,3072]{0,1:T(8,128)(2,1)} copy(bf16[1024,3072]{1,0:T(8,128)(2,1)} %all-gather.5.cloned.1.call-done) | data formatting | bytes 12582912 | tf_op jit(solution)/shard_map/all_gather | solution.py:126
  154.6 9.3 %fusion.8 = bf16[128,24,128]{0,2,1:T(8,128)(2,1)S(1)} fusion(bf16[1024,24,128]{0,2,1:T(8,128)(2,1)} %bitcast.404, f32[24,128,1024]{2,1,0:T(8,128)} %copy-done.2, f32[24,128]{1,0:T(8,128)S(1)} %broadcast_maximum_fusion, f32[128,24]{0,1:T(8,128)S(1)} %bitcast.468), kind=kOutput, calls=%fused_computation.48 | convolution fusion | flops 815529984 | bytes 19685376 | tf_op jit(solution)/shard_map/hqk,khd->hqd/dot_general | solution.py:56
  164.1 1.6 copy.28
  165.8 1.7 fusion.7
  167.9 8.3 %all-reduce.38 = (bf16[128,64]{0,1:T(8,128)(2,1)S(1)}, bf16[128]{0:T(256)(128)(2,1)S(1)}) all-reduce(bf16[128,64]{0,1:T(8,128)(2,1)S(1)} %convolution_convert_fusion, bf16[128]{0:T(256)(128)(2,1)S(1)} %get-tuple-element.14), channel_id=1, replica_groups=mesh['groups'=2,'seq'=4,'head'=2,'rep'=2] {'head'}, use_global_device_ids=true, to_apply=%region_2.0 | all-reduce | flops 8320 | bytes 33280 | tf_op jit(solution)/shard_map/psum | solution.py:137
  (126 shorter events, 17.4 us)
Async XLA Ops:
  7.2 85.5 %copy-start = (bf16[128,3072]{1,0:T(8,128)(2,1)S(1)}, bf16[128,3072]{1,0:T(8,128)(2,1)}, u32[]{:S(2)}) copy-start(bf16[128,3072]{1,0:T(8,128)(2,1)} %param.11) | copy-start | bytes 2359300
  7.2 85.5 %all-gather.3.cloned.1.call-start = ((), (), s32[]{:S(2)}) async-start(), calls=%async_computation | async-start | bytes 7077888 | tf_op jit(solution)/shard_map/all_gather | solution.py:125
  9.6 136.3 %all-gather.5.cloned.1.call-start = ((), (), s32[]{:S(2)}) async-start(), calls=%async_computation.1 | async-start | bytes 7077888 | tf_op jit(solution)/shard_map/all_gather | solution.py:126
  27.4 17.6 %collective-permute-start.1 = (bf16[128,2,1,128]{0,3,1,2:T(8,128)(2,1)S(1)}, bf16[128,2,1,128]{0,3,1,2:T(8,128)(2,1)S(1)}, u32[]{:S(2)}, u32[]{:S(2)}) collective-permute-start(bf16[128,2,1,128]{0,3,1,2:T(8,128)(2,1)S(1)} %bitcast.461), channel_id=1, source_target_pairs={{4,0},{8,4},{12,8},{5,1},{9,5},{13,9},{6,2},{10,6},{14,10},{7,3},{... | collective-permute-start | bytes 196616 | tf_op jit(solution)/shard_map/ppermute | solution.py:24
  28.7 16.3 %collective-permute-start = (bf16[128,2,1,128]{0,3,1,2:T(8,128)(2,1)S(1)}, bf16[128,2,1,128]{0,3,1,2:T(8,128)(2,1)S(1)}, u32[]{:S(2)}, u32[]{:S(2)}) collective-permute-start(bf16[128,2,1,128]{0,3,1,2:T(8,128)(2,1)S(1)} %bitcast.462), channel_id=1, source_target_pairs={{0,4},{4,8},{8,12},{1,5},{5,9},{9,13},{2,6},{6,10},{10,14},{3,7},{... | collective-permute-start | bytes 196616 | tf_op jit(solution)/shard_map/ppermute | solution.py:23
  53.7 2.3 %slice-start = ((s8[7077888]{0:T(1024)(128)(4,1)}), s8[4194304]{0:T(1024)(128)(4,1)S(1)}, s32[]{:S(2)}) async-start(s8[7077888]{0:T(1024)(128)(4,1)} %bitcast.402), calls=%async_computation.2 | async-start | bytes 8388608
  54.2 2.8 %slice-start.1 = ((s8[7077888]{0:T(1024)(128)(4,1)}), s8[2883584]{0:T(1024)(128)(4,1)S(1)}, s32[]{:S(2)}) async-start(s8[7077888]{0:T(1024)(128)(4,1)} %bitcast.402), calls=%async_computation.3 | async-start | bytes 5767168
  63.5 11.6 %collective-permute-start.3 = (bf16[128,2,1,128]{0,3,1,2:T(8,128)(2,1)S(1)}, bf16[128,2,1,128]{0,3,1,2:T(8,128)(2,1)S(1)}, u32[]{:S(2)}, u32[]{:S(2)}) collective-permute-start(bf16[128,2,1,128]{0,3,1,2:T(8,128)(2,1)S(1)} %bitcast.464), channel_id=1, source_target_pairs={{4,0},{8,4},{12,8},{5,1},{9,5},{13,9},{6,2},{10,6},{14,10},{7,3},{... | collective-permute-start | bytes 196616 | tf_op jit(solution)/shard_map/ppermute | solution.py:24
  64.8 10.3 %collective-permute-start.2 = (bf16[128,2,1,128]{0,3,1,2:T(8,128)(2,1)S(1)}, bf16[128,2,1,128]{0,3,1,2:T(8,128)(2,1)S(1)}, u32[]{:S(2)}, u32[]{:S(2)}) collective-permute-start(bf16[128,2,1,128]{0,3,1,2:T(8,128)(2,1)S(1)} %bitcast.465), channel_id=1, source_target_pairs={{0,4},{4,8},{8,12},{1,5},{5,9},{9,13},{2,6},{6,10},{10,14},{3,7},{... | collective-permute-start | bytes 196616 | tf_op jit(solution)/shard_map/ppermute | solution.py:23
  97.4 4.5 %copy-start.2 = (f32[24,128,1024]{2,1,0:T(8,128)}, f32[24,128,1024]{2,1,0:T(8,128)S(1)}, u32[]{:S(2)}) copy-start(f32[24,128,1024]{2,1,0:T(8,128)S(1)} %get-tuple-element.71) | copy-start | bytes 37748740
  154.6 11.2 %copy-start.3 = (bf16[128,3072]{1,0:T(8,128)(2,1)S(1)}, bf16[128,3072]{1,0:T(8,128)(2,1)}, u32[]{:S(2)}) copy-start(bf16[128,3072]{1,0:T(8,128)(2,1)} %param.14) | copy-start | bytes 2359300
  154.6 22.2 %copy-start.1 = (bf16[128,3072]{1,0:T(8,128)(2,1)S(1)}, bf16[128,3072]{1,0:T(8,128)(2,1)}, u32[]{:S(2)}) copy-start(bf16[128,3072]{1,0:T(8,128)(2,1)} %param.11) | copy-start | bytes 2359300
  163.9 3.6 %copy-start.5 = (bf16[3072,64]{0,1:T(8,128)(2,1)S(1)}, bf16[3072,64]{0,1:T(8,128)(2,1)}, u32[]{:S(2)}) copy-start(bf16[3072,64]{0,1:T(8,128)(2,1)} %param.16) | copy-start | bytes 1179652
  164.0 3.6 %copy-start.6 = (f32[3072]{0:T(1024)S(1)}, f32[3072]{0:T(1024)}, u32[]{:S(2)}) copy-start(f32[3072]{0:T(1024)} %param.15) | copy-start | bytes 36868
  167.5 9.3 %copy-start.4 = (bf16[128,3072]{1,0:T(8,128)(2,1)}, bf16[128,3072]{1,0:T(8,128)(2,1)S(1)}, u32[]{:S(2)}) copy-start(bf16[128,3072]{1,0:T(8,128)(2,1)S(1)} %get-tuple-element.15) | copy-start | bytes 2359300
Sparse Core Ops, SparseCore 0:
  10.2 70.7 all-gather.2
  82.6 63.2 all-gather.4
where the time goes:
time: 184 us
  waiting for transfers between devices  53.9 us (29%)
  blocking collectives  40.7 us (22%)
  matrix products  28.4 us (15%)
  local copies, waits for them, and re-layouts  23.8 us (13%)
  starting transfers between devices  16.6 us (9%)
  between operations  14.9 us (8%)
  other arithmetic  5.36 us (3%)
    all_gather x1, waiting for transfers between devices, shards(): lax.all_gather(value_tokens, ('seq', 'rep'), axis=0, tiled=True)  41.2 us
    all_gather x2, blocking collectives, shards(): rimmed = lax.all_gather(bordered, ('head', 'rep'), axis=0, tiled=True)  17.3 us
    all_gather x1, blocking collectives, shards(): lax.all_gather(tile_pool, 'seq', axis=0, tiled=True)  15.2 us
    ppermute x2, starting transfers between devices, padded(): before = lax.ppermute(last, axis, up)  14 us
    ppermute x2, waiting for transfers between devices, padded(): after = lax.ppermute(leading, axis, down)  12.6 us
    dot_general x54, matrix products, tap_sum(): lax.dot_general(tap_weight, window.reshape(piece_rows, -1), (((1,), (0,))...  12.2 us
    unnamed x21, local copies, waits for them, and re-layouts  10.4 us
    dot_general x1, matrix products, make_update(): jnp.einsum('hqk,khd->hqd', exponent.astype(jnp.bfloat16), value_heads, pr...  9.31 us
  transfers between devices with their start and end apart: 6, of which 3 were waited for; matrix products, arithmetic and copies ran while one was open for 14% of the time, Pallas kernels for 0%

commit v1 on v0

--- a/solution.py
+++ b/solution.py
@@ -1,8 +1,11 @@
+import functools
 import math
 
 import jax
 import jax.numpy as jnp
 from jax import lax
+from jax.experimental import pallas as pl
+from jax.experimental.pallas import tpu as pltpu
 from jax.sharding import PartitionSpec as P
 
 HEAD_DIM = 128
@@ -104,6 +107,186 @@
     return jnp.einsum("tp,plfc->lftc", selector, piece_block, preferred_element_type=jnp.float32)
 
 
+MESH = pl.DeviceIdType.MESH
+
+
+def fused_kernel(
+    seq_size, rep_size, head_size,
+    q_ref, k_ref, v_ref, stream_ref, gain_ref, lw_ref,
+    hid_ref, lat_ref,
+    qkv, obuf, att, part, part_in,
+    send_sem, recv_sem, osend_sem, orecv_sem, psend_sem, precv_sem,
+):
+    seq, rep, head = (lax.axis_index(a) for a in ("seq", "rep", "head"))
+    count = seq_size * rep_size
+    me = seq * rep_size + rep
+    rows = q_ref.shape[0]
+    own_heads = qkv.shape[0]
+    others = count - 1
+    factor = 1.0 / math.sqrt(HEAD_DIM)
+    offsets = [(d, e) for d in (2, 1, 3, 0) for e in range(rep_size) if (d, e) != (0, 0)]
+
+    def peer(d, e):
+        return lax.rem(seq + d, seq_size), lax.rem(rep + e, rep_size)
+
+    partner = {"head": lax.rem(head + 1, head_size)}
+    barrier = pltpu.get_barrier_semaphore()
+    for d, e in offsets:
+        ps, pr = peer(d, e)
+        pl.semaphore_signal(barrier, inc=1, device_id={"seq": ps, "rep": pr}, device_id_type=MESH)
+    pl.semaphore_signal(barrier, inc=1, device_id=partner, device_id_type=MESH)
+    pl.semaphore_wait(barrier, others + 1)
+
+    my_rows = pl.ds(pl.multiple_of(me * rows, rows), rows)
+    sources = (q_ref, k_ref, v_ref)
+    for h in range(own_heads):
+        for d, e in offsets:
+            ps, pr = peer(d, e)
+            column = ((ps * rep_size + pr) * own_heads + h) * HEAD_DIM
+            columns = pl.ds(pl.multiple_of(column, HEAD_DIM), HEAD_DIM)
+            for a, source in enumerate(sources):
+                pltpu.make_async_remote_copy(
+                    src_ref=source.at[:, columns],
+                    dst_ref=qkv.at[h, a, my_rows, :],
+                    send_sem=send_sem,
+                    recv_sem=recv_sem.at[h],
+                    device_id={"seq": ps, "rep": pr},
+                    device_id_type=MESH,
+                ).start()
+    for h in range(own_heads):
+        columns = pl.ds(pl.multiple_of((me * own_heads + h) * HEAD_DIM, HEAD_DIM), HEAD_DIM)
+        for a, source in enumerate(sources):
+            qkv[h, a, my_rows, :] = source[:, columns]
+
+    def arrived(ref, sem):
+        pltpu.make_async_copy(ref, ref, sem).wait()
+
+    block = rep_size * rows
+    for h in range(own_heads):
+        arrived(qkv.at[h, :, pl.ds(0, others * rows), :], recv_sem.at[h])
+        out_columns = pl.ds(pl.multiple_of((me * own_heads + h) * HEAD_DIM, HEAD_DIM), HEAD_DIM)
+
+        def attend(step, carry):
+            target = lax.rem(seq + 2 + step, seq_size)
+            here = pl.ds(pl.multiple_of(target * block, block), block)
+            scores = lax.dot_general(
+                qkv[h, 0, here, :], qkv[h, 1], (((1,), (1,)), ((), ())),
+                preferred_element_type=jnp.float32,
+            ) * factor
+            exponent = jnp.exp(scores - jnp.max(scores, axis=1, keepdims=True))
+            total = jnp.sum(exponent, axis=1, keepdims=True)
+            summed = jnp.dot(
+                exponent.astype(jnp.bfloat16), qkv[h, 2], preferred_element_type=jnp.float32
+            )
+            obuf[h, here, :] = (summed / total).astype(jnp.bfloat16)
+            for r in range(rep_size):
+                @pl.when(jnp.logical_or(target != seq, rep != r))
+                def _():
+                    start = pl.multiple_of(target * block + r * rows, rows)
+                    pltpu.make_async_remote_copy(
+                        src_ref=obuf.at[h, pl.ds(start, rows), :],
+                        dst_ref=att.at[:, out_columns],
+                        send_sem=osend_sem,
+                        recv_sem=orecv_sem.at[h],
+                        device_id={"seq": target, "rep": r},
+                        device_id_type=MESH,
+                    ).start()
+            return carry
+
+        lax.fori_loop(0, seq_size, attend, 0)
+        att[:, out_columns] = obuf[h, my_rows, :]
+
+    squares = jnp.zeros((rows, HEAD_DIM), jnp.float32)
+    projected = jnp.zeros((rows, lw_ref.shape[0]), jnp.float32)
+    for h in range(own_heads):
+        arrived(obuf.at[h, pl.ds(0, others * rows), :], orecv_sem.at[h])
+        for j in range(count):
+            low = (j * own_heads + h) * HEAD_DIM
+            cols = slice(low, low + HEAD_DIM)
+            combined = stream_ref[:, cols].astype(jnp.float32) + att[:, cols].astype(jnp.float32)
+            hidden = combined.astype(jnp.bfloat16)
+            hid_ref[:, cols] = hidden
+            widened = hidden.astype(jnp.float32)
+            squares = squares + widened * widened
+            scaled = (widened * gain_ref[:, cols]).astype(jnp.bfloat16)
+            projected = projected + lax.dot_general(
+                scaled, lw_ref[:, cols], (((1,), (1,)), ((), ())),
+                preferred_element_type=jnp.float32,
+            )
+    latent = projected.shape[1]
+    summed = jnp.sum(squares, axis=1, keepdims=True)
+    part[:, :latent] = projected
+    part[:, latent:] = jnp.broadcast_to(summed, (rows, part.shape[1] - latent))
+    swap = pltpu.make_async_remote_copy(
+        src_ref=part, dst_ref=part_in, send_sem=psend_sem, recv_sem=precv_sem,
+        device_id=partner, device_id_type=MESH,
+    )
+    swap.start()
+    arrived(qkv.at[:, :, pl.ds(0, others * rows), :], send_sem)
+    arrived(obuf.at[:, pl.ds(0, others * rows), :], osend_sem)
+    swap.wait()
+    both = part[...] + part_in[...]
+    width = q_ref.shape[1] * head_size
+    lat_ref[...] = both[:, :latent] * lax.rsqrt(both[:, latent:latent + 1] / width + epsilon)
+
+
+def fused(queries, key_tokens, value_tokens, stream, norm_gain, latent_weight):
+    seq_size, rep_size, head_size = (lax.axis_size(a) for a in ("seq", "rep", "head"))
+    rows, width = queries.shape
+    count = seq_size * rep_size
+    own_heads = width // HEAD_DIM // count
+    latent = latent_weight.shape[1]
+    lanes = 2 * latent
+    bf = jnp.bfloat16
+    vmem = pl.BlockSpec(memory_space=pltpu.VMEM)
+    dma = pltpu.SemaphoreType.DMA
+    return pl.pallas_call(
+        functools.partial(fused_kernel, seq_size, rep_size, head_size),
+        out_shape=(
+            jax.ShapeDtypeStruct((rows, width), bf),
+            jax.ShapeDtypeStruct((rows, latent), jnp.float32),
+        ),
+        in_specs=[vmem] * 6,
+        out_specs=(vmem, vmem),
+        scratch_shapes=[
+            pltpu.VMEM((own_heads, 3, count * rows, HEAD_DIM), bf),
+            pltpu.VMEM((own_heads, count * rows, HEAD_DIM), bf),
+            pltpu.VMEM((rows, width), bf),
+            pltpu.VMEM((rows, lanes), jnp.float32),
+            pltpu.VMEM((rows, lanes), jnp.float32),
+            dma, dma((own_heads,)), dma, dma((own_heads,)), dma, dma,
+        ],
+        compiler_params=pltpu.CompilerParams(
+            collective_id=0, has_side_effects=True, vmem_limit_bytes=48 << 20
+        ),
+    )(queries, key_tokens, value_tokens, stream, norm_gain[None, :], latent_weight.T)
+
+
+def gathered(queries, key_tokens, value_tokens, stream, norm_gain, latent_weight):
+    query_heads, initial = prepare(queries)
+    state = make_update(
+        query_heads,
+        initial,
+        (
+            lax.all_gather(key_tokens, ("seq", "rep"), axis=0, tiled=True),
+            lax.all_gather(value_tokens, ("seq", "rep"), axis=0, tiled=True),
+        ),
+    )
+    attended = finish(state)
+    combined = stream.astype(jnp.float32) + attended.astype(jnp.float32)
+    hidden = combined.astype(jnp.bfloat16)
+    widened = hidden.astype(jnp.float32)
+    scaled = (widened * norm_gain).astype(jnp.bfloat16)
+    partial_proj = jnp.dot(scaled, latent_weight, preferred_element_type=jnp.float32)
+    partial_squares = jnp.sum(widened * widened, axis=1)
+    projected, squares = (
+        lax.psum(partial_proj.astype(jnp.bfloat16), "head").astype(jnp.float32),
+        lax.psum(partial_squares.astype(jnp.bfloat16), "head").astype(jnp.float32),
+    )
+    latents = projected * lax.rsqrt(squares / WIDTH + epsilon)[:, None]
+    return hidden, latents
+
+
 def shards(
     queries,
     key_tokens,
@@ -117,27 +300,13 @@
     lift_bias,
     conv_weight,
 ):
-    query_heads, initial = prepare(queries)
-    state = make_update(
-        query_heads,
-        initial,
-        (
-            lax.all_gather(key_tokens, ("seq", "rep"), axis=0, tiled=True),
-            lax.all_gather(value_tokens, ("seq", "rep"), axis=0, tiled=True),
-        ),
-    )
-    attended = finish(state)
-    combined = stream.astype(jnp.float32) + attended.astype(jnp.float32)
-    hidden = combined.astype(jnp.bfloat16)
-    widened = hidden.astype(jnp.float32)
-    scaled = (widened * norm_gain).astype(jnp.bfloat16)
-    partial_proj = jnp.dot(scaled, latent_weight, preferred_element_type=jnp.float32)
-    partial_squares = jnp.sum(widened * widened, axis=1)
-    projected, squares = (
-        lax.psum(partial_proj.astype(jnp.bfloat16), "head").astype(jnp.float32),
-        lax.psum(partial_squares.astype(jnp.bfloat16), "head").astype(jnp.float32),
-    )
-    latents = projected * lax.rsqrt(squares / WIDTH + epsilon)[:, None]
+    heads_here = queries.shape[1] // HEAD_DIM
+    spread = lax.axis_size("seq") * lax.axis_size("rep")
+    fits = heads_here % spread == 0 and lax.axis_size("seq") == 4 and lax.axis_size("head") == 2
+    attention = fused if fits else gathered
+    hidden, latents = attention(
+        queries, key_tokens, value_tokens, stream, norm_gain, latent_weight
+    )
     tiles_here = tile_pool.shape[0]
     frames = tile_pool.shape[2]
     columns = tile_pool.shape[3]

time: 184 us -> 171 us (0.929)
  Pallas kernels: 0 us -> 76 us
  waiting for transfers between devices: 53.9 us -> 4.86 us
  local copies, waits for them, and re-layouts: 23.8 us -> 7.72 us
  between operations: 14.9 us -> 1.55 us
  matrix products: 28.4 us -> 38.2 us
  blocking collectives: 40.7 us -> 32.7 us
  starting transfers between devices: 16.6 us -> 9.22 us
  other arithmetic: 5.36 us -> 0.08 us
    pallas_call x0 -> x1, Pallas kernels: none -> 76 us  [fused(): pl.pallas_call(functools.partial(fused_kernel, seq_size, rep_size, head_s...]
    all_gather x2 -> x0, waiting for transfers between devices: 41.2 us -> none  [the longest x1 41.2 us: shards(): lax.all_gather(value_tokens, ('seq', 'rep'), axis=0, tiled=True)]
    dot_general x54, matrix products: 12.2 us -> 36.5 us  [tap_sum(): lax.dot_general(tap_weight, window.reshape(piece_rows, -1), (((1,), (0,))...]
    dot_general x3 -> x0, matrix products: 14.4 us -> none  [the longest x1 9.31 us: make_update(): jnp.einsum('hqk,khd->hqd', exponent.astype(jnp.bfloat16), value_heads, pr...]
    all_gather x1 -> x0, local copies, waits for them, and re-layouts: 8.73 us -> none  [shards(): lax.all_gather(value_tokens, ('seq', 'rep'), axis=0, tiled=True)]
    ppermute x2, waiting for transfers between devices: 12.6 us -> 4.28 us  [padded(): after = lax.ppermute(leading, axis, down)]
    psum x1 -> x0, blocking collectives: 8.27 us -> none  [shards(): lax.psum(partial_proj.astype(jnp.bfloat16), 'head').astype(jnp.float32)]
    ppermute x2, starting transfers between devices: 14 us -> 6.63 us  [padded(): before = lax.ppermute(last, axis, up)]
  transfers between devices with their start and end apart: 6 -> 4, of which waited for: 3 -> 2; matrix products, arithmetic and copies ran while one was open for 14% -> 0% of each run, Pallas kernels for 0% -> 45%
where the time goes in v1:
time: 171 us; the launch traced here: 170 us
  Pallas kernels  76 us (44%)
  matrix products  38.2 us (22%)
  blocking collectives  32.7 us (19%)
  starting transfers between devices  9.22 us (5%)
  local copies, waits for them, and re-layouts  7.72 us (5%)
  waiting for transfers between devices  4.86 us (3%)
    pallas_call x1, Pallas kernels, fused(): pl.pallas_call(functools.partial(fused_kernel, seq_size, rep_size, head_s...  76 us
    dot_general x54, matrix products, tap_sum(): lax.dot_general(tap_weight, window.reshape(piece_rows, -1), (((1,), (0,))...  36.5 us
    all_gather x2, blocking collectives, shards(): rimmed = lax.all_gather(bordered, ('head', 'rep'), axis=0, tiled=True)  17.6 us
    all_gather x1, blocking collectives, shards(): lax.all_gather(tile_pool, 'seq', axis=0, tiled=True)  15.1 us
    ppermute x2, starting transfers between devices, padded(): before = lax.ppermute(last, axis, up)  6.63 us
    unnamed x22, local copies, waits for them, and re-layouts  4.67 us
    ppermute x2, waiting for transfers between devices, padded(): after = lax.ppermute(leading, axis, down)  4.28 us
  transfers between devices with their start and end apart: 4, of which 2 were waited for; matrix products, arithmetic and copies ran while one was open for 0% of the time, Pallas kernels for 45%

profile of v1, /device:TPU:0, one launch (start us, length us, event | category | flops | bytes accessed | tf_op | source)
XLA Modules:
  0.0 170.4 jit_solution(1862951561413435557)
XLA Ops:
  1.4 15.1 %all_gather.9 = bf16[4,64,2,128]{3,1,2,0:T(8,128)(2,1)S(1)} all-gather(bf16[1,64,2,128]{3,1,2,0:T(8,128)(2,1)S(1)} %copy.16), channel_id=1, replica_groups=mesh['groups'=2,'seq'=4,'head'=2,'rep'=2] {'seq'}, dimensions={0}, use_global_device_ids=true | all-gather | bytes 163840 | tf_op jit(solution)/shard_map/all_gather | solution.py:315
  18.3 3.8 %collective-permute-start = (bf16[128,2,1,128]{0,3,1,2:T(8,128)(2,1)S(1)}, bf16[128,2,1,128]{0,3,1,2:T(8,128)(2,1)S(1)}, u32[]{:S(2)}, u32[]{:S(2)}) collective-permute-start(bf16[128,2,1,128]{0,3,1,2:T(8,128)(2,1)S(1)} %bitcast.444), channel_id=1, source_target_pairs={{0,4},{4,8},{8,12},{1,5},{5,9},{9,13},{2,6},{6,10},{10,14},{3,7},{... | collective-permute-start | bytes 196616 | tf_op jit(solution)/shard_map/ppermute | solution.py:26
  22.1 1.3 collective-permute-start.1
  23.9 4.3 %collective-permute-done.1 = bf16[128,2,1,128]{0,3,1,2:T(8,128)(2,1)S(1)} collective-permute-done((bf16[128,2,1,128]{0,3,1,2:T(8,128)(2,1)S(1)}, bf16[128,2,1,128]{0,3,1,2:T(8,128)(2,1)S(1)}, u32[]{:S(2)}, u32[]{:S(2)}) %collective-permute-start.1) | collective-permute-done | bytes 65568 | tf_op jit(solution)/shard_map/ppermute | solution.py:27
  28.3 8.6 %all_gather.10 = bf16[512,2,3,128]{0,3,1,2:T(8,128)(2,1)S(1)} all-gather(bf16[128,2,3,128]{0,3,1,2:T(8,128)(2,1)S(1)} %pad_maximum_fusion), channel_id=1, replica_groups=mesh['groups'=2,'seq'=4,'head'=2,'rep'=2] {'head','rep'}, dimensions={0}, use_global_device_ids=true | all-gather | bytes 983040 | tf_op jit(solution)/shard_map/all_gather | solution.py:337
  38.7 1.4 slice-done.1
  46.4 2.9 %collective-permute-start.2 = (bf16[128,2,1,128]{0,3,1,2:T(8,128)(2,1)S(1)}, bf16[128,2,1,128]{0,3,1,2:T(8,128)(2,1)S(1)}, u32[]{:S(2)}, u32[]{:S(2)}) collective-permute-start(bf16[128,2,1,128]{0,3,1,2:T(8,128)(2,1)S(1)} %bitcast.441), channel_id=1, source_target_pairs={{0,4},{4,8},{8,12},{1,5},{5,9},{9,13},{2,6},{6,10},{10,14},{3,7},{... | collective-permute-start | bytes 196616 | tf_op jit(solution)/shard_map/ppermute | solution.py:26
  49.2 1.3 collective-permute-start.3
  50.6 76.0 %shard_map.130 = (bf16[128,3072]{1,0:T(8,128)(2,1)S(1)}, f32[128,64]{1,0:T(8,128)S(1)}) custom-call(bf16[128,3072]{1,0:T(8,128)(2,1)S(1)} %copy-done.1, bf16[128,3072]{1,0:T(8,128)(2,1)S(1)} %copy-done.2, bf16[128,3072]{1,0:T(8,128)(2,1)S(1)} %copy-done.3, bf16[128,3072]{1,0:T(8,128)(2,1)S(1)} %copy-done.4, f32[1,3072]{1,0:T(1,128)S(1)} %bitcast.382, ...), custom_call_target="tpu_custom_call" | custom-call | tf_op jit(solution)/shard_map/pallas_call | solution.py:243
  127.3 9.0 %all_gather.11 = bf16[512,2,3,128]{0,3,1,2:T(8,128)(2,1)S(1)} all-gather(bf16[128,2,3,128]{0,3,1,2:T(8,128)(2,1)S(1)} %pad_maximum_fusion.1), channel_id=1, replica_groups=mesh['groups'=2,'seq'=4,'head'=2,'rep'=2] {'head','rep'}, dimensions={0}, use_global_device_ids=true | all-gather | bytes 983040 | tf_op jit(solution)/shard_map/all_gather | solution.py:337
  137.2 1.1 fusion.51
  139.2 1.1 convolution_add_fusion.15
  141.4 1.1 convolution_add_fusion.13
  143.7 1.1 convolution_add_fusion.11
  146.0 1.1 convolution_add_fusion.9
  148.3 1.1 convolution_add_fusion.7
  150.5 1.1 convolution_add_fusion.5
  152.8 1.1 convolution_add_fusion.3
  155.1 1.1 convolution_add_fusion.1
  157.3 1.1 fusion.10
  159.6 1.1 fusion.8
  161.9 1.1 fusion.6
  164.2 1.1 fusion.4
  166.4 1.1 fusion.2
  (110 shorter events, 29.4 us)
Async XLA Ops:
  0.6 16.8 %copy-start = (bf16[64,128]{1,0:T(8,128)(2,1)S(1)}, bf16[64,128]{1,0:T(8,128)(2,1)}, u32[]{:S(2)}) copy-start(bf16[64,128]{1,0:T(8,128)(2,1)} %param.19) | copy-start | bytes 49156
  18.3 5.7 %collective-permute-start = (bf16[128,2,1,128]{0,3,1,2:T(8,128)(2,1)S(1)}, bf16[128,2,1,128]{0,3,1,2:T(8,128)(2,1)S(1)}, u32[]{:S(2)}, u32[]{:S(2)}) collective-permute-start(bf16[128,2,1,128]{0,3,1,2:T(8,128)(2,1)S(1)} %bitcast.444), channel_id=1, source_target_pairs={{0,4},{4,8},{8,12},{1,5},{5,9},{9,13},{2,6},{6,10},{10,14},{3,7},{... | collective-permute-start | bytes 196616 | tf_op jit(solution)/shard_map/ppermute | solution.py:26
  22.1 6.2 %collective-permute-start.1 = (bf16[128,2,1,128]{0,3,1,2:T(8,128)(2,1)S(1)}, bf16[128,2,1,128]{0,3,1,2:T(8,128)(2,1)S(1)}, u32[]{:S(2)}, u32[]{:S(2)}) collective-permute-start(bf16[128,2,1,128]{0,3,1,2:T(8,128)(2,1)S(1)} %bitcast.445), channel_id=1, source_target_pairs={{4,0},{8,4},{12,8},{5,1},{9,5},{13,9},{6,2},{10,6},{14,10},{7,3},{... | collective-permute-start | bytes 196616 | tf_op jit(solution)/shard_map/ppermute | solution.py:27
  36.9 1.8 %slice-start = ((s8[7077888]{0:T(1024)(128)(4,1)}), s8[2883584]{0:T(1024)(128)(4,1)S(1)}, s32[]{:S(2)}) async-start(s8[7077888]{0:T(1024)(128)(4,1)} %bitcast.383), calls=%async_computation | async-start | bytes 5767168
  37.4 2.7 %slice-start.1 = ((s8[7077888]{0:T(1024)(128)(4,1)}), s8[4194304]{0:T(1024)(128)(4,1)S(1)}, s32[]{:S(2)}) async-start(s8[7077888]{0:T(1024)(128)(4,1)} %bitcast.383), calls=%async_computation.1 | async-start | bytes 8388608
  41.4 9.1 %copy-start.1 = (bf16[128,3072]{1,0:T(8,128)(2,1)S(1)}, bf16[128,3072]{1,0:T(8,128)(2,1)}, u32[]{:S(2)}) copy-start(bf16[128,3072]{1,0:T(8,128)(2,1)} %q_ref.1) | copy-start | bytes 2359300
  41.5 9.1 %copy-start.2 = (bf16[128,3072]{1,0:T(8,128)(2,1)S(1)}, bf16[128,3072]{1,0:T(8,128)(2,1)}, u32[]{:S(2)}) copy-start(bf16[128,3072]{1,0:T(8,128)(2,1)} %k_ref.1) | copy-start | bytes 2359300
  41.5 9.1 %copy-start.3 = (bf16[128,3072]{1,0:T(8,128)(2,1)S(1)}, bf16[128,3072]{1,0:T(8,128)(2,1)}, u32[]{:S(2)}) copy-start(bf16[128,3072]{1,0:T(8,128)(2,1)} %v_ref.1) | copy-start | bytes 2359300
  41.5 9.1 %copy-start.4 = (bf16[128,3072]{1,0:T(8,128)(2,1)S(1)}, bf16[128,3072]{1,0:T(8,128)(2,1)}, u32[]{:S(2)}) copy-start(bf16[128,3072]{1,0:T(8,128)(2,1)} %stream_ref.1) | copy-start | bytes 2359300
  41.5 9.1 %copy-start.5 = (bf16[3072,64]{0,1:T(8,128)(2,1)S(1)}, bf16[3072,64]{0,1:T(8,128)(2,1)}, u32[]{:S(2)}) copy-start(bf16[3072,64]{0,1:T(8,128)(2,1)} %param.16) | copy-start | bytes 1179652
  41.5 9.1 %copy-start.6 = (f32[3072]{0:T(1024)S(1)}, f32[3072]{0:T(1024)}, u32[]{:S(2)}) copy-start(f32[3072]{0:T(1024)} %param.15) | copy-start | bytes 36868
  46.4 80.9 %collective-permute-start.2 = (bf16[128,2,1,128]{0,3,1,2:T(8,128)(2,1)S(1)}, bf16[128,2,1,128]{0,3,1,2:T(8,128)(2,1)S(1)}, u32[]{:S(2)}, u32[]{:S(2)}) collective-permute-start(bf16[128,2,1,128]{0,3,1,2:T(8,128)(2,1)S(1)} %bitcast.441), channel_id=1, source_target_pairs={{0,4},{4,8},{8,12},{1,5},{5,9},{9,13},{2,6},{6,10},{10,14},{3,7},{... | collective-permute-start | bytes 196616 | tf_op jit(solution)/shard_map/ppermute | solution.py:26
  49.2 78.1 %collective-permute-start.3 = (bf16[128,2,1,128]{0,3,1,2:T(8,128)(2,1)S(1)}, bf16[128,2,1,128]{0,3,1,2:T(8,128)(2,1)S(1)}, u32[]{:S(2)}, u32[]{:S(2)}) collective-permute-start(bf16[128,2,1,128]{0,3,1,2:T(8,128)(2,1)S(1)} %bitcast.442), channel_id=1, source_target_pairs={{4,0},{8,4},{12,8},{5,1},{9,5},{13,9},{6,2},{10,6},{14,10},{7,3},{... | collective-permute-start | bytes 196616 | tf_op jit(solution)/shard_map/ppermute | solution.py:27

commit v2 on v1

--- a/solution.py
+++ b/solution.py
@@ -113,9 +113,12 @@
 def fused_kernel(
     seq_size, rep_size, head_size,
     q_ref, k_ref, v_ref, stream_ref, gain_ref, lw_ref,
-    hid_ref, lat_ref,
+    tile_ref, pick_ref, lift_ref, bias_ref, conv_ref,
+    hid_ref, lat_ref, dec_ref,
     qkv, obuf, att, part, part_in,
+    tiles, lifts, biases, taps, act1, act2, feat, acc,
     send_sem, recv_sem, osend_sem, orecv_sem, psend_sem, precv_sem,
+    tap_sem, dsend_sem, drecv_sem,
 ):
     seq, rep, head = (lax.axis_index(a) for a in ("seq", "rep", "head"))
     count = seq_size * rep_size
@@ -130,12 +133,40 @@
         return lax.rem(seq + d, seq_size), lax.rem(rep + e, rep_size)
 
     partner = {"head": lax.rem(head + 1, head_size)}
+    mates = [
+        {"head": lax.rem(head + d, head_size), "rep": lax.rem(rep + e, rep_size)}
+        for d in range(head_size) for e in range(rep_size) if (d, e) != (0, 0)
+    ]
+    quarter = head * rep_size + rep
+    tap_copy = pltpu.make_async_copy(conv_ref, taps, tap_sem)
+    tap_copy.start()
     barrier = pltpu.get_barrier_semaphore()
     for d, e in offsets:
         ps, pr = peer(d, e)
         pl.semaphore_signal(barrier, inc=1, device_id={"seq": ps, "rep": pr}, device_id_type=MESH)
-    pl.semaphore_signal(barrier, inc=1, device_id=partner, device_id_type=MESH)
-    pl.semaphore_wait(barrier, others + 1)
+    strangers = [m for m, e in zip(mates, range(1, head_size * rep_size)) if e >= rep_size]
+    for mate in strangers:
+        pl.semaphore_signal(barrier, inc=1, device_id=mate, device_id_type=MESH)
+    pl.semaphore_wait(barrier, others + len(strangers))
+
+    def arrived(ref, sem):
+        pltpu.make_async_copy(ref, ref, sem).wait()
+
+    def send(source, target, index, device):
+        pltpu.make_async_remote_copy(
+            src_ref=source, dst_ref=target,
+            send_sem=dsend_sem.at[index], recv_sem=drecv_sem.at[index],
+            device_id=device, device_id_type=MESH,
+        ).start()
+
+    share = tile_ref.shape[0] // (head_size * rep_size)
+    my_share = pl.ds(pl.multiple_of(quarter * share, share), share)
+    for d in range(1, seq_size):
+        send(tile_ref.at[my_share, :], tiles.at[seq, my_share, :], 0,
+             {"seq": lax.rem(seq + d, seq_size)})
+    for mate in mates:
+        send(lift_ref, lifts.at[quarter], 1, mate)
+        send(bias_ref, biases.at[quarter], 2, mate)
 
     my_rows = pl.ds(pl.multiple_of(me * rows, rows), rows)
     sources = (q_ref, k_ref, v_ref)
@@ -158,8 +189,94 @@
         for a, source in enumerate(sources):
             qkv[h, a, my_rows, :] = source[:, columns]
 
-    def arrived(ref, sem):
-        pltpu.make_async_copy(ref, ref, sem).wait()
+    tiles[seq, my_share, :] = tile_ref[my_share, :]
+    lifts[quarter] = lift_ref[...]
+    biases[quarter] = bias_ref[...]
+    pieces = len(mates)
+    arrived(tiles.at[pl.ds(0, seq_size - 1), pl.ds(0, share), :], drecv_sem.at[0])
+    for mate in mates:
+        send(tiles.at[:, my_share, :], tiles.at[:, my_share, :], 3, mate)
+    arrived(lifts.at[pl.ds(0, pieces)], drecv_sem.at[1])
+    arrived(biases.at[pl.ds(0, pieces)], drecv_sem.at[2])
+    arrived(tiles.at[:, pl.ds(0, pieces * share), :], drecv_sem.at[3])
+
+    frames, reach, columns_here, channels = act1.shape
+    own = lift_ref.shape[1]
+    margin = reach // 2
+    own_lanes = pl.ds(pl.multiple_of(quarter * own, own), own)
+
+    def inside(d):
+        row = seq + d
+        return jnp.where(jnp.logical_and(row >= 0, row < seq_size), 1.0, 0.0)
+
+    def silu(value):
+        return value / (1.0 + jnp.exp(-value))
+
+    def lifted(chosen, weight, bias):
+        return lax.dot_general(
+            chosen, weight, (((0,), (0,)), ((), ())), preferred_element_type=jnp.float32
+        ) + bias
+
+    for d in range(reach):
+        chosen = jnp.zeros(tile_ref.shape, jnp.float32)
+        for p in range(seq_size):
+            chosen = chosen + pick_ref[d, p] * tiles[p].astype(jnp.float32)
+        chosen = chosen.astype(jnp.bfloat16)
+        for c in range(pieces + 1):
+            active = silu(lifted(chosen, lifts[c], biases[c, :1, :])) * inside(d - margin)
+            act1[:, d, :, c * own:(c + 1) * own] = active.astype(jnp.bfloat16).reshape(
+                frames, columns_here, own
+            )
+        if 1 <= d <= reach - 2:
+            feat[:, d - 1] = lifted(chosen, lift_ref[...], bias_ref[:1, :]).reshape(
+                frames, columns_here, own
+            )
+
+    def convolve(layer, active, rows_out):
+        length = rows_out * columns_here
+        for f in range(frames):
+            first = True
+            for a in range(3):
+                if not 0 <= f + a - 1 < frames:
+                    continue
+                for b in range(3):
+                    window = active[f + a - 1, b:b + rows_out].reshape(length, channels)
+                    base = 9 * a + 3 * b
+                    term = lax.dot_general(
+                        window, taps[layer, base:base + 3].reshape(3 * own, channels),
+                        (((1,), (1,)), ((), ())), preferred_element_type=jnp.float32,
+                    )
+                    acc[f, :length, :] = term if first else acc[f, :length, :] + term
+                    first = False
+
+    def gathered_columns(f, r):
+        lines = slice(r * columns_here, (r + 1) * columns_here)
+        at = lax.broadcasted_iota(jnp.int32, (columns_here, own), 0)
+        before = pltpu.roll(acc[f, lines, :own], 1, 0)
+        after = pltpu.roll(acc[f, lines, 2 * own:], columns_here - 1, 0)
+        return (
+            acc[f, lines, own:2 * own]
+            + jnp.where(at == 0, 0.0, before)
+            + jnp.where(at == columns_here - 1, 0.0, after)
+        )
+
+    tap_copy.wait()
+    convolve(0, act1, reach - 2)
+    for f in range(frames):
+        for r in range(reach - 2):
+            value = feat[f, r] + gathered_columns(f, r)
+            feat[f, r] = value
+            act2[f, r, :, own_lanes] = (silu(value) * inside(r + 1 - margin)).astype(jnp.bfloat16)
+    for mate in mates:
+        send(act2.at[:, :, :, own_lanes], act2.at[:, :, :, own_lanes], 4, mate)
+
+    def last_layer():
+        arrived(act2.at[:, :, :, pl.ds(0, pieces * own)], drecv_sem.at[4])
+        convolve(1, act2, reach - 4)
+        for f in range(frames):
+            dec_ref[f * columns_here:(f + 1) * columns_here, :] = (
+                feat[f, margin - 1] + gathered_columns(f, 0)
+            )
 
     block = rep_size * rows
     for h in range(own_heads):
@@ -195,6 +312,8 @@
 
         lax.fori_loop(0, seq_size, attend, 0)
         att[:, out_columns] = obuf[h, my_rows, :]
+        if h == 0:
+            last_layer()
 
     squares = jnp.zeros((rows, HEAD_DIM), jnp.float32)
     projected = jnp.zeros((rows, lw_ref.shape[0]), jnp.float32)
@@ -225,41 +344,72 @@
     arrived(qkv.at[:, :, pl.ds(0, others * rows), :], send_sem)
     arrived(obuf.at[:, pl.ds(0, others * rows), :], osend_sem)
     swap.wait()
+    arrived(tiles.at[pl.ds(0, seq_size - 1), pl.ds(0, share), :], dsend_sem.at[0])
+    arrived(lifts.at[pl.ds(0, pieces)], dsend_sem.at[1])
+    arrived(biases.at[pl.ds(0, pieces)], dsend_sem.at[2])
+    arrived(tiles.at[:, pl.ds(0, pieces * share), :], dsend_sem.at[3])
+    arrived(act2.at[:, :, :, pl.ds(0, pieces * own)], dsend_sem.at[4])
     both = part[...] + part_in[...]
     width = q_ref.shape[1] * head_size
     lat_ref[...] = both[:, :latent] * lax.rsqrt(both[:, latent:latent + 1] / width + epsilon)
 
 
-def fused(queries, key_tokens, value_tokens, stream, norm_gain, latent_weight):
+def fused(
+    queries, key_tokens, value_tokens, stream, norm_gain, latent_weight,
+    tile_pool, tile_position, lift_weight, lift_bias, conv_weight,
+):
     seq_size, rep_size, head_size = (lax.axis_size(a) for a in ("seq", "rep", "head"))
     rows, width = queries.shape
     count = seq_size * rep_size
     own_heads = width // HEAD_DIM // count
     latent = latent_weight.shape[1]
     lanes = 2 * latent
+    depth, frames, columns = tile_pool.shape[1:]
+    layers, _, own, channels = conv_weight.shape
+    quarters = head_size * rep_size
+    reach = 2 * layers + 1
     bf = jnp.bfloat16
     vmem = pl.BlockSpec(memory_space=pltpu.VMEM)
+    smem = pl.BlockSpec(memory_space=pltpu.SMEM)
     dma = pltpu.SemaphoreType.DMA
-    return pl.pallas_call(
+    grid_rows = lax.axis_index("seq") + jnp.arange(reach, dtype=jnp.int32) - layers
+    pick = (grid_rows[:, None] == tile_position[None, :]).astype(jnp.float32)
+    hidden, latents, decoded = pl.pallas_call(
         functools.partial(fused_kernel, seq_size, rep_size, head_size),
         out_shape=(
             jax.ShapeDtypeStruct((rows, width), bf),
             jax.ShapeDtypeStruct((rows, latent), jnp.float32),
+            jax.ShapeDtypeStruct((frames * columns, own), jnp.float32),
         ),
-        in_specs=[vmem] * 6,
-        out_specs=(vmem, vmem),
+        in_specs=[vmem] * 7 + [smem, vmem, vmem, pl.BlockSpec(memory_space=pl.ANY)],
+        out_specs=(vmem, vmem, vmem),
         scratch_shapes=[
             pltpu.VMEM((own_heads, 3, count * rows, HEAD_DIM), bf),
             pltpu.VMEM((own_heads, count * rows, HEAD_DIM), bf),
             pltpu.VMEM((rows, width), bf),
             pltpu.VMEM((rows, lanes), jnp.float32),
             pltpu.VMEM((rows, lanes), jnp.float32),
+            pltpu.VMEM((seq_size, depth, frames * columns), bf),
+            pltpu.VMEM((quarters, depth, own), bf),
+            pltpu.VMEM((quarters, 8, own), jnp.float32),
+            pltpu.VMEM(conv_weight.shape, bf),
+            pltpu.VMEM((frames, reach, columns, channels), bf),
+            pltpu.VMEM((frames, reach - 2, columns, channels), bf),
+            pltpu.VMEM((frames, reach - 2, columns, own), jnp.float32),
+            pltpu.VMEM((frames, (reach - 2) * columns, 3 * own), jnp.float32),
             dma, dma((own_heads,)), dma, dma((own_heads,)), dma, dma,
+            dma, dma((5,)), dma((5,)),
         ],
         compiler_params=pltpu.CompilerParams(
-            collective_id=0, has_side_effects=True, vmem_limit_bytes=48 << 20
+            collective_id=0, has_side_effects=True, vmem_limit_bytes=56 << 20
         ),
-    )(queries, key_tokens, value_tokens, stream, norm_gain[None, :], latent_weight.T)
+    )(
+        queries, key_tokens, value_tokens, stream, norm_gain[None, :], latent_weight.T,
+        tile_pool[0].reshape(depth, frames * columns), pick, lift_weight,
+        jnp.broadcast_to(lift_bias[None, :], (8, own)), conv_weight,
+    )
+    decoded = decoded.reshape(frames, columns, own).transpose(2, 0, 1)[:, :, None, :]
+    return hidden, latents, decoded
 
 
 def gathered(queries, key_tokens, value_tokens, stream, norm_gain, latent_weight):
@@ -303,8 +453,14 @@
     heads_here = queries.shape[1] // HEAD_DIM
     spread = lax.axis_size("seq") * lax.axis_size("rep")
     fits = heads_here % spread == 0 and lax.axis_size("seq") == 4 and lax.axis_size("head") == 2
-    attention = fused if fits else gathered
-    hidden, latents = attention(
+    fits = fits and lax.axis_size("rep") == 2 and tile_pool.shape[0] == 1
+    fits = fits and conv_weight.shape[0] == 2 and lift_weight.shape[0] % 64 == 0
+    if fits:
+        return fused(
+            queries, key_tokens, value_tokens, stream, norm_gain, latent_weight,
+            tile_pool, tile_position, lift_weight, lift_bias, conv_weight,
+        )
+    hidden, latents = gathered(
         queries, key_tokens, value_tokens, stream, norm_gain, latent_weight
     )
     tiles_here = tile_pool.shape[0]

time: 171 us -> 90.8 us (0.53)
  matrix products: 38.2 us -> 0 us
  blocking collectives: 32.7 us -> 0 us
  starting transfers between devices: 9.22 us -> 0 us
  waiting for transfers between devices: 4.86 us -> 0 us
  Pallas kernels: 76 us -> 80.6 us
    dot_general x56 -> x0, matrix products: 38.2 us -> none  [the longest x54 36.5 us: tap_sum(): lax.dot_general(tap_weight, window.reshape(piece_rows, -1), (((1,), (0,))...]
    all_gather x3 -> x0, blocking collectives: 32.7 us -> none  [the longest x2 17.6 us: shards(): rimmed = lax.all_gather(bordered, ('head', 'rep'), axis=0, tiled=True)]
    ppermute x4 -> x0, starting transfers between devices: 9.22 us -> none  [the longest x2 6.63 us: padded(): before = lax.ppermute(last, axis, up)]
    ppermute x4 -> x0, waiting for transfers between devices: 4.86 us -> none  [the longest x2 4.28 us: padded(): after = lax.ppermute(leading, axis, down)]
    pallas_call x1, Pallas kernels: 76 us -> 80.6 us  [fused(): pl.pallas_call(functools.partial(fused_kernel, seq_size, rep_size, head_s...]
    unnamed x22 -> x3, local copies, waits for them, and re-layouts: 4.67 us -> 4.98 us
  transfers between devices with their start and end apart: 4 -> 0, of which waited for: 2 -> 0; matrix products, arithmetic and copies ran while one was open for 0% -> 0% of each run, Pallas kernels for 45% -> 0%
where the time goes in v2:
time: 90.8 us; the launch traced here: 90.5 us
  Pallas kernels  80.6 us (89%)
  local copies, waits for them, and re-layouts  7.88 us (9%)
  other arithmetic  1.32 us (1%)
    pallas_call x1, Pallas kernels, fused(): pl.pallas_call(functools.partial(fused_kernel, seq_size, rep_size, head_s...  80.6 us
    unnamed x3, local copies, waits for them, and re-layouts  4.98 us

profile of v2, /device:TPU:0, one launch (start us, length us, event | category | flops | bytes accessed | tf_op | source)
XLA Modules:
  0.0 90.5 jit_solution(17427514650608243419)
XLA Ops:
  0.6 1.3 %compare_convert_fusion.pick_ref = f32[5,4]{1,0:T(8,128)} fusion(s32[4]{0:T(128)} %param.18, s32[5]{0:T(128)S(1)} %add_add_fusion), kind=kLoop, calls=%fused_computation.1 | loop fusion | flops 40 | bytes 116 | tf_op jit(solution)/shard_map/convert_element_type | solution.py:376
  2.0 1.2 %broadcast_in_dim.7.bias_ref = f32[8,128]{1,0:T(8,128)} broadcast(f32[128]{0:T(128)} %param.20), dimensions={1} | broadcast | bytes 4608 | tf_op jit(solution)/shard_map/broadcast_in_dim | solution.py:409
  3.2 1.4 %copy.18 = bf16[8,8,2,128]{3,1,2,0:T(8,128)(2,1)} copy(bf16[8,8,2,128]{3,2,1,0:T(2,128)(2,1)} %bitcast.15) | data formatting | bytes 65536
  4.6 80.6 %shard_map.130 = (bf16[128,3072]{1,0:T(8,128)(2,1)}, f32[128,64]{1,0:T(8,128)}, f32[256,128]{1,0:T(8,128)}) custom-call(bf16[128,3072]{1,0:T(8,128)(2,1)} %q_ref.1, bf16[128,3072]{1,0:T(8,128)(2,1)} %k_ref.1, bf16[128,3072]{1,0:T(8,128)(2,1)} %v_ref.1, bf16[128,3072]{1,0:T(8,128)(2,1)} %stream_ref.1, f32[1,3072]{1,0:T(1,128)} %bitcast.16, ...), custom_call_target="tpu_custom_call" | custom-call | tf_op jit(solution)/shard_map/pallas_call | solution.py:377
  85.2 1.5 %copy.15 = f32[128,64]{0,1:T(8,128)} copy(f32[128,64]{1,0:T(8,128)} %get-tuple-element.10) | data formatting | bytes 65536
  86.8 1.7 %copy.14 = f32[2,128,128]{1,0,2:T(2,128)} copy(f32[2,128,128]{2,1,0:T(8,128)} %bitcast.14) | data formatting | bytes 262144 | tf_op jit(solution)/shard_map/reshape | solution.py:411
  88.4 2.1 %copy.20 = bf16[128,3072]{1,0:T(8,128)(2,1)} copy(bf16[128,3072]{1,0:T(8,128)(2,1)} %get-tuple-element.15) | data formatting | bytes 1572864
  (1 shorter events, 0.0 us)

commit v3 on v2

--- a/solution.py
+++ b/solution.py
@@ -112,14 +112,23 @@
 
 def fused_kernel(
     seq_size, rep_size, head_size,
-    q_ref, k_ref, v_ref, stream_ref, gain_ref, lw_ref,
-    tile_ref, pick_ref, lift_ref, bias_ref, conv_ref,
-    hid_ref, lat_ref, dec_ref,
+    q_hbm, k_hbm, v_hbm, stream_hbm, gain_ref, lw_ref,
+    tile_ref, place_ref, lift_ref, bias_ref, conv_ref,
+    hid_hbm, sums_ref, dec_ref,
+    q_ref, k_ref, v_ref, stream_ref, hid_ref,
     qkv, obuf, att, part, part_in,
     tiles, lifts, biases, taps, act1, act2, feat, acc,
     send_sem, recv_sem, osend_sem, orecv_sem, psend_sem, precv_sem,
-    tap_sem, dsend_sem, drecv_sem,
+    load_sem, hid_sem, tap_sem, dsend_sem, drecv_sem,
 ):
+    loads = [
+        pltpu.make_async_copy(source, target, load_sem.at[i])
+        for i, (source, target) in enumerate(
+            ((q_hbm, q_ref), (k_hbm, k_ref), (v_hbm, v_ref), (stream_hbm, stream_ref))
+        )
+    ]
+    for load in loads:
+        load.start()
     seq, rep, head = (lax.axis_index(a) for a in ("seq", "rep", "head"))
     count = seq_size * rep_size
     me = seq * rep_size + rep
@@ -159,15 +168,17 @@
             device_id=device, device_id_type=MESH,
         ).start()
 
-    share = tile_ref.shape[0] // (head_size * rep_size)
+    share = tile_ref.shape[1] // (head_size * rep_size)
     my_share = pl.ds(pl.multiple_of(quarter * share, share), share)
     for d in range(1, seq_size):
-        send(tile_ref.at[my_share, :], tiles.at[seq, my_share, :], 0,
+        send(tile_ref.at[0, my_share], tiles.at[seq, my_share], 0,
              {"seq": lax.rem(seq + d, seq_size)})
     for mate in mates:
         send(lift_ref, lifts.at[quarter], 1, mate)
         send(bias_ref, biases.at[quarter], 2, mate)
 
+    for load in loads[:3]:
+        load.wait()
     my_rows = pl.ds(pl.multiple_of(me * rows, rows), rows)
     sources = (q_ref, k_ref, v_ref)
     for h in range(own_heads):
@@ -189,16 +200,16 @@
         for a, source in enumerate(sources):
             qkv[h, a, my_rows, :] = source[:, columns]
 
-    tiles[seq, my_share, :] = tile_ref[my_share, :]
+    tiles[seq, my_share] = tile_ref[0, my_share]
     lifts[quarter] = lift_ref[...]
     biases[quarter] = bias_ref[...]
     pieces = len(mates)
-    arrived(tiles.at[pl.ds(0, seq_size - 1), pl.ds(0, share), :], drecv_sem.at[0])
+    arrived(tiles.at[pl.ds(0, seq_size - 1), pl.ds(0, share)], drecv_sem.at[0])
     for mate in mates:
-        send(tiles.at[:, my_share, :], tiles.at[:, my_share, :], 3, mate)
+        send(tiles.at[:, my_share], tiles.at[:, my_share], 3, mate)
     arrived(lifts.at[pl.ds(0, pieces)], drecv_sem.at[1])
     arrived(biases.at[pl.ds(0, pieces)], drecv_sem.at[2])
-    arrived(tiles.at[:, pl.ds(0, pieces * share), :], drecv_sem.at[3])
+    arrived(tiles.at[:, pl.ds(0, pieces * share)], drecv_sem.at[3])
 
     frames, reach, columns_here, channels = act1.shape
     own = lift_ref.shape[1]
@@ -217,20 +228,18 @@
             chosen, weight, (((0,), (0,)), ((), ())), preferred_element_type=jnp.float32
         ) + bias
 
+    wide = [tiles[p].astype(jnp.float32) for p in range(seq_size)]
     for d in range(reach):
-        chosen = jnp.zeros(tile_ref.shape, jnp.float32)
+        picked = jnp.zeros(wide[0].shape, jnp.float32)
         for p in range(seq_size):
-            chosen = chosen + pick_ref[d, p] * tiles[p].astype(jnp.float32)
-        chosen = chosen.astype(jnp.bfloat16)
-        for c in range(pieces + 1):
-            active = silu(lifted(chosen, lifts[c], biases[c, :1, :])) * inside(d - margin)
-            act1[:, d, :, c * own:(c + 1) * own] = active.astype(jnp.bfloat16).reshape(
-                frames, columns_here, own
-            )
-        if 1 <= d <= reach - 2:
-            feat[:, d - 1] = lifted(chosen, lift_ref[...], bias_ref[:1, :]).reshape(
-                frames, columns_here, own
-            )
+            picked = picked + jnp.where(place_ref[p] == seq + d - margin, 1.0, 0.0) * wide[p]
+        for f in range(frames):
+            chosen = picked[:, f, :].astype(jnp.bfloat16)
+            for c in range(pieces + 1):
+                active = silu(lifted(chosen, lifts[c], biases[c])) * inside(d - margin)
+                act1[f, d, :, c * own:(c + 1) * own] = active.astype(jnp.bfloat16)
+            if 1 <= d <= reach - 2:
+                feat[f, d - 1] = lifted(chosen, lift_ref[...], bias_ref[...])
 
     def convolve(layer, active, rows_out):
         length = rows_out * columns_here
@@ -315,6 +324,7 @@
         if h == 0:
             last_layer()
 
+    loads[3].wait()
     squares = jnp.zeros((rows, HEAD_DIM), jnp.float32)
     projected = jnp.zeros((rows, lw_ref.shape[0]), jnp.float32)
     for h in range(own_heads):
@@ -341,17 +351,49 @@
         device_id=partner, device_id_type=MESH,
     )
     swap.start()
+    hid_copy = pltpu.make_async_copy(hid_ref, hid_hbm, hid_sem)
+    hid_copy.start()
     arrived(qkv.at[:, :, pl.ds(0, others * rows), :], send_sem)
     arrived(obuf.at[:, pl.ds(0, others * rows), :], osend_sem)
     swap.wait()
-    arrived(tiles.at[pl.ds(0, seq_size - 1), pl.ds(0, share), :], dsend_sem.at[0])
+    arrived(tiles.at[pl.ds(0, seq_size - 1), pl.ds(0, share)], dsend_sem.at[0])
     arrived(lifts.at[pl.ds(0, pieces)], dsend_sem.at[1])
     arrived(biases.at[pl.ds(0, pieces)], dsend_sem.at[2])
-    arrived(tiles.at[:, pl.ds(0, pieces * share), :], dsend_sem.at[3])
+    arrived(tiles.at[:, pl.ds(0, pieces * share)], dsend_sem.at[3])
     arrived(act2.at[:, :, :, pl.ds(0, pieces * own)], dsend_sem.at[4])
-    both = part[...] + part_in[...]
-    width = q_ref.shape[1] * head_size
-    lat_ref[...] = both[:, :latent] * lax.rsqrt(both[:, latent:latent + 1] / width + epsilon)
+    sums_ref[...] = part[...] + part_in[...]
+    hid_copy.wait()
+
+
+def finish_kernel(
+    full_width, hid_in, sums_ref, dec_in, hid_out, lat_ref, dec_ref, held, in_sem, out_sem
+):
+    chunks = held.shape[0]
+    size = hid_in.shape[0] // chunks
+    reads = [
+        pltpu.make_async_copy(hid_in.at[pl.ds(i * size, size), :], held.at[i], in_sem.at[i])
+        for i in range(chunks)
+    ]
+    writes = [
+        pltpu.make_async_copy(held.at[i], hid_out.at[pl.ds(i * size, size), :], out_sem.at[i])
+        for i in range(chunks)
+    ]
+    for read in reads:
+        read.start()
+    for read, write in zip(reads, writes):
+        read.wait()
+        write.start()
+    latent = lat_ref.shape[0]
+    sums = jnp.transpose(sums_ref[...])
+    lat_ref[...] = sums[:latent] * lax.rsqrt(sums[latent:latent + 1] / full_width + epsilon)
+    frames = dec_ref.shape[0] // dec_in.shape[1]
+    columns = dec_in.shape[0] // frames
+    for f in range(frames):
+        dec_ref[pl.ds(f, dec_in.shape[1], stride=frames), :] = jnp.transpose(
+            dec_in[f * columns:(f + 1) * columns, :]
+        )
+    for write in writes:
+        write.wait()
 
 
 def fused(
@@ -370,46 +412,57 @@
     reach = 2 * layers + 1
     bf = jnp.bfloat16
     vmem = pl.BlockSpec(memory_space=pltpu.VMEM)
+    hbm = pl.BlockSpec(memory_space=pltpu.HBM)
     smem = pl.BlockSpec(memory_space=pltpu.SMEM)
     dma = pltpu.SemaphoreType.DMA
-    grid_rows = lax.axis_index("seq") + jnp.arange(reach, dtype=jnp.int32) - layers
-    pick = (grid_rows[:, None] == tile_position[None, :]).astype(jnp.float32)
-    hidden, latents, decoded = pl.pallas_call(
+    hidden, sums, decoded = pl.pallas_call(
         functools.partial(fused_kernel, seq_size, rep_size, head_size),
         out_shape=(
             jax.ShapeDtypeStruct((rows, width), bf),
-            jax.ShapeDtypeStruct((rows, latent), jnp.float32),
+            jax.ShapeDtypeStruct((rows, lanes), jnp.float32),
             jax.ShapeDtypeStruct((frames * columns, own), jnp.float32),
         ),
-        in_specs=[vmem] * 7 + [smem, vmem, vmem, pl.BlockSpec(memory_space=pl.ANY)],
-        out_specs=(vmem, vmem, vmem),
-        scratch_shapes=[
+        in_specs=[hbm] * 4 + [vmem] * 3 + [smem, vmem, vmem, hbm],
+        out_specs=(hbm, vmem, vmem),
+        scratch_shapes=[pltpu.VMEM((rows, width), bf)] * 5 + [
             pltpu.VMEM((own_heads, 3, count * rows, HEAD_DIM), bf),
             pltpu.VMEM((own_heads, count * rows, HEAD_DIM), bf),
             pltpu.VMEM((rows, width), bf),
             pltpu.VMEM((rows, lanes), jnp.float32),
             pltpu.VMEM((rows, lanes), jnp.float32),
-            pltpu.VMEM((seq_size, depth, frames * columns), bf),
+            pltpu.VMEM((seq_size, depth, frames, columns), bf),
             pltpu.VMEM((quarters, depth, own), bf),
-            pltpu.VMEM((quarters, 8, own), jnp.float32),
+            pltpu.VMEM((quarters, 1, own), jnp.float32),
             pltpu.VMEM(conv_weight.shape, bf),
             pltpu.VMEM((frames, reach, columns, channels), bf),
             pltpu.VMEM((frames, reach - 2, columns, channels), bf),
             pltpu.VMEM((frames, reach - 2, columns, own), jnp.float32),
             pltpu.VMEM((frames, (reach - 2) * columns, 3 * own), jnp.float32),
             dma, dma((own_heads,)), dma, dma((own_heads,)), dma, dma,
-            dma, dma((5,)), dma((5,)),
+            dma((4,)), dma, dma, dma((5,)), dma((5,)),
         ],
         compiler_params=pltpu.CompilerParams(
             collective_id=0, has_side_effects=True, vmem_limit_bytes=56 << 20
         ),
     )(
         queries, key_tokens, value_tokens, stream, norm_gain[None, :], latent_weight.T,
-        tile_pool[0].reshape(depth, frames * columns), pick, lift_weight,
-        jnp.broadcast_to(lift_bias[None, :], (8, own)), conv_weight,
-    )
-    decoded = decoded.reshape(frames, columns, own).transpose(2, 0, 1)[:, :, None, :]
-    return hidden, latents, decoded
+        tile_pool, tile_position, lift_weight, lift_bias[None, :], conv_weight,
+    )
+    chunks = 4
+    hidden, latents, decoded = pl.pallas_call(
+        functools.partial(finish_kernel, width * head_size),
+        out_shape=(
+            jax.ShapeDtypeStruct((rows, width), bf),
+            jax.ShapeDtypeStruct((latent, rows), jnp.float32),
+            jax.ShapeDtypeStruct((own * frames, columns), jnp.float32),
+        ),
+        in_specs=[hbm, vmem, vmem],
+        out_specs=(hbm, vmem, vmem),
+        scratch_shapes=[
+            pltpu.VMEM((chunks, rows // chunks, width), bf), dma((chunks,)), dma((chunks,)),
+        ],
+    )(hidden, sums, decoded)
+    return hidden, latents.T, decoded.reshape(own, frames, 1, columns)
 
 
 def gathered(queries, key_tokens, value_tokens, stream, norm_gain, latent_weight):

time: 90.8 us -> 84.1 us (0.926)
  local copies, waits for them, and re-layouts: 7.88 us -> 0 us
  Pallas kernels: 80.6 us -> 83.2 us
  other arithmetic: 1.32 us -> 0 us
    unnamed x3 -> x0, local copies, waits for them, and re-layouts: 4.98 us -> none
    pallas_call x0 -> x1, Pallas kernels: none -> 3.57 us  [fused(): pl.pallas_call(functools.partial(finish_kernel, width * head_size), out_s...]
    reshape x1 -> x0, local copies, waits for them, and re-layouts: 1.66 us -> none  [fused(): decoded.reshape(frames, columns, own).transpose(2, 0, 1)[:, :, None, :]]
    convert_element_type x1 -> x0, other arithmetic: 1.32 us -> none  [fused(): pick = (grid_rows[:, None] == tile_position[None, :]).astype(jnp.float32)]
    broadcast_in_dim x1 -> x0, local copies, waits for them, and re-layouts: 1.25 us -> none  [fused(): jnp.broadcast_to(lift_bias[None, :], (8, own))]
    pallas_call x1, Pallas kernels: 80.6 us -> 79.7 us  [fused(): pl.pallas_call(functools.partial(fused_kernel, seq_size, rep_size, head_s...]
where the time goes in v3:
time: 84.1 us; the launch traced here: 83.9 us
  Pallas kernels  83.2 us (99%)
    pallas_call x1, Pallas kernels, fused(): pl.pallas_call(functools.partial(fused_kernel, seq_size, rep_size, head_s...  79.7 us
    pallas_call x1, Pallas kernels, fused(): pl.pallas_call(functools.partial(finish_kernel, width * head_size), out_s...  3.57 us

profile of v3, /device:TPU:0, one launch (start us, length us, event | category | flops | bytes accessed | tf_op | source)
XLA Modules:
  0.0 83.9 jit_solution(5429484943382164530)
XLA Ops:
  0.6 79.7 %shard_map.130 = (bf16[128,3072]{1,0:T(8,128)(2,1)}, f32[128,128]{1,0:T(8,128)}, f32[256,128]{1,0:T(8,128)}) custom-call(bf16[128,3072]{1,0:T(8,128)(2,1)} %q_hbm.1, bf16[128,3072]{1,0:T(8,128)(2,1)} %k_hbm.1, bf16[128,3072]{1,0:T(8,128)(2,1)} %v_hbm.1, bf16[128,3072]{1,0:T(8,128)(2,1)} %stream_hbm.1, f32[1,3072]{1,0:T(1,128)} %bitcast.8, ...), custom_call_target="tpu_custom_call" | custom-call | tf_op jit(solution)/shard_map/pallas_call | solution.py:418
  80.3 3.6 %shard_map.131 = (bf16[128,3072]{1,0:T(8,128)(2,1)}, f32[64,128]{1,0:T(8,128)}, f32[256,128]{1,0:T(8,128)}) custom-call(bf16[128,3072]{1,0:T(8,128)(2,1)} %get-tuple-element.9.hid_in, f32[128,128]{1,0:T(8,128)} %get-tuple-element.10.sums_ref, f32[256,128]{1,0:T(8,128)} %get-tuple-element.11.dec_in), custom_call_target="tpu_custom_call" | custom-call | tf_op jit(solution)/shard_map/pallas_call | solution.py:452

commit v4 on v3

--- a/solution.py
+++ b/solution.py
@@ -321,7 +321,7 @@
 
         lax.fori_loop(0, seq_size, attend, 0)
         att[:, out_columns] = obuf[h, my_rows, :]
-        if h == 0:
+        if h == own_heads - 1:
             last_layer()
 
     loads[3].wait()

time: 84.1 us -> 84.1 us (level)
  no operation moved by 1% of the time
where the time goes in v4:
time: 84.1 us; the launch traced here: 83.9 us
  Pallas kernels  83.2 us (99%)
    pallas_call x1, Pallas kernels, fused(): pl.pallas_call(functools.partial(fused_kernel, seq_size, rep_size, head_s...  79.7 us
    pallas_call x1, Pallas kernels, fused(): pl.pallas_call(functools.partial(finish_kernel, width * head_size), out_s...  3.57 us

profile of v4, /device:TPU:0, one launch (start us, length us, event | category | flops | bytes accessed | tf_op | source)
XLA Modules:
  0.0 83.9 jit_solution(10263709028540336745)
XLA Ops:
  0.6 79.7 %shard_map.130 = (bf16[128,3072]{1,0:T(8,128)(2,1)}, f32[128,128]{1,0:T(8,128)}, f32[256,128]{1,0:T(8,128)}) custom-call(bf16[128,3072]{1,0:T(8,128)(2,1)} %q_hbm.1, bf16[128,3072]{1,0:T(8,128)(2,1)} %k_hbm.1, bf16[128,3072]{1,0:T(8,128)(2,1)} %v_hbm.1, bf16[128,3072]{1,0:T(8,128)(2,1)} %stream_hbm.1, f32[1,3072]{1,0:T(1,128)} %bitcast.8, ...), custom_call_target="tpu_custom_call" | custom-call | tf_op jit(solution)/shard_map/pallas_call | solution.py:418
  80.3 3.6 %shard_map.131 = (bf16[128,3072]{1,0:T(8,128)(2,1)}, f32[64,128]{1,0:T(8,128)}, f32[256,128]{1,0:T(8,128)}) custom-call(bf16[128,3072]{1,0:T(8,128)(2,1)} %get-tuple-element.9.hid_in, f32[128,128]{1,0:T(8,128)} %get-tuple-element.10.sums_ref, f32[256,128]{1,0:T(8,128)} %get-tuple-element.11.dec_in), custom_call_target="tpu_custom_call" | custom-call | tf_op jit(solution)/shard_map/pallas_call | solution.py:452
